TPU v7x, 256 devices: a whole 4x4x8 slice. The times are simulated.
256 devices in a mesh: section: 2 (over core), dp: 16 (over z, x_lo), tensor: 8 (over y, x_hi).
Axes of the slice: x: 4 (x_hi: 2, x_lo: 2; x = x_hi * 2 + x_lo), y: 4, z: 8, core: 2. Of those that a mesh axis runs over, the one named last changes fastest.
Arguments:
- tokens: bfloat16 [2048, 4096], P('dp', 'tensor'), may hold values from -6 to 6
- gain: bfloat16 [2, 4096], P('section', 'tensor'), may hold values from 0.099609375 to 1.8984375
- w_up: bfloat16 [2, 4096, 5120], P('section', 'dp', 'tensor'), may hold values from -0.09375 to 0.09375
- w_down: bfloat16 [2, 5120, 4096], P('section', 'tensor', 'dp'), may hold values from -0.078125 to 0.078125
- cotangent: bfloat16 [2, 2048, 4096], P('section', 'dp'), may hold values from -6 to 6
Outputs:
- states: bfloat16 [2, 2048, 4096], P('section', 'dp', 'tensor')
- grad_down: bfloat16 [2, 5120, 4096], P('section', 'tensor', 'dp')
All inputs are finite; a program needn't handle non-finite values.
Results may differ from a plain program's by a relative error of at most 0.02.
Values may be sent and summed in bfloat16 or wider, within the bound.
No kernel may reach another device: no remote copies, remote signals or barrier semaphores. Data moves between devices by JAX's collectives and lax.ppermute only.
A program may use at most 64 MiB of HBM per device.

v0:
```python
import jax
import jax.numpy as jnp
from jax import lax
from jax.sharding import Mesh
from jax.sharding import PartitionSpec as P

MICRO = 2
MB_ROWS = 64
DP = ("dp_0", "dp_1")
EPS = 1e-06


def gathered_by_axis(array, axes, dim):
    filled = array
    for number in range(len(axes) - 1, -1, -1):
        filled = lax.all_gather(filled, axes[number], axis=dim, tiled=True)
    return filled


def in_order(pieces, dim):
    dims = list(pieces.shape[1:])
    dims[dim] *= pieces.shape[0]
    return jnp.moveaxis(pieces, 0, dim).reshape(dims)


def copy_for_each(array, axis):
    peers = lax.axis_size(axis)
    return lax.all_to_all(
        jnp.broadcast_to(array[None], (peers, *array.shape)), axis, 0, 0, tiled=True
    )


def collect(array, axis, dim):
    return in_order(copy_for_each(array, axis), dim)


def split_up(array, dim, peers):
    before, after = (array.shape[:dim], array.shape[dim + 1 :])
    return jnp.moveaxis(array.reshape(*before, peers, -1, *after), dim, 0)


def summed_on_arrival(array, axis, dim):
    pieces = split_up(array, dim, lax.axis_size(axis))
    arrived = lax.all_to_all(pieces, axis, split_axis=0, concat_axis=0, tiled=True)
    return arrived.astype(jnp.float32).sum(axis=0)


def shifted(array, axis, by):
    peers = lax.axis_size(axis)
    pairs = [(i, i + by) for i in range(peers) if 0 <= i + by < peers]
    return lax.ppermute(array, axis, pairs)


def body(tokens, gain, w_up, w_down, cotangent):
    section_id = lax.axis_index("section")
    section_count = lax.axis_size("section")
    up_whole = gathered_by_axis(w_up[0], DP, 0)
    down_whole = gathered_by_axis(w_down[0], DP, 1)
    width = up_whole.shape[0]
    hidden_width = up_whole.shape[1]
    gain_own = gain[0]
    gain_whole = lax.all_gather(gain_own, "tensor", axis=0, tiled=True)
    micro_rows = MB_ROWS
    micro_count = MICRO
    own_width = tokens.shape[1]
    tok_rows = tokens.shape[0]

    def project(normed):
        pre_act = jnp.dot(normed, up_whole, preferred_element_type=jnp.float32)
        hidden = jax.nn.gelu(pre_act, approximate=True).astype(jnp.bfloat16)
        partial_value = jnp.dot(hidden, down_whole, preferred_element_type=jnp.float32).astype(
            jnp.bfloat16
        )
        return (hidden, lax.optimization_barrier(partial_value).astype(jnp.float32))

    def skipped(normed):
        return (
            jnp.zeros((micro_rows, hidden_width), jnp.bfloat16),
            jnp.zeros((micro_rows, width), jnp.float32),
        )

    def advance(step_id, loop_state):
        incoming, states, hiddens = loop_state
        micro_id = step_id - section_id
        active = (micro_id >= 0) & (micro_id < micro_count)
        slot_pos = jnp.clip(micro_id, 0, micro_count - 1) * micro_rows
        entry_rows = lax.dynamic_slice_in_dim(tokens, slot_pos, micro_rows, 0)
        current = jnp.where(section_id == 0, entry_rows, incoming)
        current_f = current.astype(jnp.float32)
        whole_rows = collect(current, "tensor", 1)
        whole_f = whole_rows.astype(jnp.float32)
        inverse_rms = lax.rsqrt(jnp.mean(whole_f * whole_f, axis=1, keepdims=True) + EPS)
        normed = (whole_f * inverse_rms * gain_whole.astype(jnp.float32)).astype(jnp.bfloat16)
        hidden, partial_value = lax.cond(active, project, skipped, normed)
        summed = summed_on_arrival(partial_value.astype(jnp.bfloat16), "tensor", 1)
        result = (current_f + summed).astype(jnp.bfloat16)
        old_state = lax.dynamic_slice_in_dim(states, slot_pos, micro_rows, 0)
        states = lax.dynamic_update_slice_in_dim(
            states, jnp.where(active, result, old_state), slot_pos, 0
        )
        old_hidden = lax.dynamic_slice_in_dim(hiddens, slot_pos, micro_rows, 0)
        hiddens = lax.dynamic_update_slice_in_dim(
            hiddens, jnp.where(active, hidden, old_hidden), slot_pos, 0
        )
        incoming = shifted(result, "section", 1)
        return (incoming, states, hiddens)

    initial = (
        jnp.zeros((micro_rows, own_width), jnp.bfloat16),
        jnp.zeros((tok_rows, own_width), jnp.bfloat16),
        jnp.zeros((tok_rows, hidden_width), jnp.bfloat16),
    )
    final_state = lax.fori_loop(0, micro_count + section_count - 1, advance, initial)
    states = final_state[1]
    hiddens = final_state[2]
    cot_own = cotangent[0]
    dp_count = lax.axis_size(DP)
    hidden_all = lax.all_gather(hiddens, DP, axis=0, tiled=True)
    cot_mine = lax.all_to_all(cot_own, DP, split_axis=1, concat_axis=0, tiled=True)
    grad_own = jnp.zeros((hidden_width, width // dp_count), jnp.float32)
    for peer_id in range(dp_count):
        lower = peer_id * tok_rows
        partial_value = lax.dot_general(
            hidden_all[lower : lower + tok_rows],
            cot_mine[lower : lower + tok_rows],
            (((0,), (0,)), ((), ())),
            preferred_element_type=jnp.float32,
        ).astype(jnp.bfloat16)
        grad_own = grad_own + lax.optimization_barrier(partial_value).astype(jnp.float32)
    return (states[None], grad_own.astype(jnp.bfloat16)[None])


def solution(mesh):
    torus = Mesh(
        mesh.devices.reshape(mesh.shape["section"], 8, 2, mesh.shape["tensor"]),
        ("section", "dp_0", "dp_1", "tensor"),
    )
    in_specs = (
        P(DP, "tensor"),
        P("section", "tensor"),
        P("section", DP, "tensor"),
        P("section", "tensor", DP),
        P("section", DP, None),
    )
    out_specs = (P("section", DP, "tensor"), P("section", "tensor", DP))
    return jax.shard_map(body, mesh=torus, in_specs=in_specs, out_specs=out_specs, check_vma=False)
```

profile of v0, /device:TPU:2, one launch (start us, length us, event | category | flops | bytes accessed | tf_op | source)
XLA Modules:
  0.0 377.0 jit_solution(14900252217565980653)
XLA Ops:
  7.2 10.4 %all-gather.1 = bf16[1,512,640]{2,1,0:T(8,128)(2,1)} all-gather(bf16[1,256,640]{2,1,0:T(8,128)(2,1)} %param.11), channel_id=3, replica_groups=mesh['section'=2,'dp_0'=8,'dp_1'=2,'tensor'=8] {'dp_1'}, dimensions={1}, use_global_device_ids=true | all-gather | bytes 983040 | tf_op jit(solution)/shard_map/all_gather | solution.py:16
  17.7 11.1 %all-gather.3 = bf16[1,640,512]{2,1,0:T(8,128)(2,1)} all-gather(bf16[1,640,256]{2,1,0:T(8,128)(2,1)} %param.12), channel_id=5, replica_groups=mesh['section'=2,'dp_0'=8,'dp_1'=2,'tensor'=8] {'dp_1'}, dimensions={2}, use_global_device_ids=true | all-gather | bytes 983040 | tf_op jit(solution)/shard_map/all_gather | solution.py:16
  29.0 31.6 %all-gather = bf16[1,4096]{1,0:T(2,128)(2,1)S(1)} all-gather(bf16[1,512]{1,0:T(2,128)(2,1)S(1)} %copy-done.7), channel_id=2, replica_groups=mesh['section'=2,'dp_0'=8,'dp_1'=2,'tensor'=8] {'tensor'}, dimensions={1}, use_global_device_ids=true | all-gather | bytes 9216 | tf_op jit(solution)/shard_map/all_gather | solution.py:62
  60.6 25.8 %all-gather.11.cloned.1.call-done = bf16[1,4096,640]{2,1,0:T(8,128)(2,1)} async-done(((bf16[1,512,640]{2,1,0:T(8,128)(2,1)}), bf16[1,4096,640]{2,1,0:T(8,128)(2,1)}) %all-gather.11.cloned.1.call-update) | async-done | bytes 5242896 | tf_op jit(solution)/shard_map/all_gather | solution.py:16
  86.5 65.0 %all-gather.13.cloned.1.call-done = bf16[1,640,4096]{2,1,0:T(8,128)(2,1)} async-done(((bf16[1,640,512]{2,1,0:T(8,128)(2,1)}), bf16[1,640,4096]{2,1,0:T(8,128)(2,1)}) %all-gather.13.cloned.1.call-update) | async-done | bytes 5242896 | tf_op jit(solution)/shard_map/all_gather | solution.py:16
  151.6 124.7 %while.18 = (s32[]{:T(128)}, bf16[64,512]{1,0:T(8,128)(2,1)S(1)}, bf16[128,512]{1,0:T(8,128)(2,1)S(1)}, bf16[128,640]{1,0:T(8,128)(2,1)S(1)}, pred[]{:T(512)}, /...) while((s32[]{:T(128)}, bf16[64,512]{1,0:T(8,128)(2,1)S(1)}, ...), condition=%wide.region_5.6_spmd, body=%wide.region_0.5_spmd.sunk | while | flops 674254912 | bytes 67036620 | solution.py:113
  151.6 0.8 broadcast_in_dim.44
  152.5 5.8 %all-to-all-start = ((bf16[8,64,512]{2,1,0:T(8,128)(2,1)}), bf16[8,64,512]{2,1,0:T(8,128)(2,1)S(1)}, u32[]{:S(2)}, u32[]{:S(2)}) async-start(bf16[8,64,512]{2,1,0:T(8,128)(2,1)} %broadcast_in_dim.44), calls=%async_computation | async-start | bytes 1048576 | tf_op jit(solution)/shard_map/while/body/eval_jaxpr/all_to_all | solution.py:28
  158.3 11.4 %all-to-all-done = bf16[8,64,512]{2,1,0:T(8,128)(2,1)S(1)} async-done(((bf16[8,64,512]{2,1,0:T(8,128)(2,1)}), bf16[8,64,512]{2,1,0:T(8,128)(2,1)S(1)}, u32[]{:S(2)}, u32[]{:S(2)}) %all-to-all-start) | async-done | bytes 524320 | tf_op jit(solution)/shard_map/while/body/eval_jaxpr/all_to_all | solution.py:28
  170.3 2.1 copy-done
  172.4 4.5 %conditional.2 = (bf16[64,640]{1,0:T(8,128)(2,1)}, bf16[64,4096]{1,0:T(8,128)(2,1)S(1)}) conditional(s32[]{:T(128)} %convert_element_type.313, () %tuple.49, (bf16[64,4096]{1,0:T(8,128)(2,1)S(1)}, bf16[4096,640]{1,0:T(8,128)(2,1)S(1)}, bf16[640,4096]{1,0:T(8,128)(2,1)}) %tuple.63), branch_computations={%region_2.2_spmd, %region_3.3_spmd} | conditional | flops 671719424 | bytes 32669740 | solution.py:94
  172.4 1.7 fusion.7
  174.1 0.9 copy-done.1
  174.9 1.9 convolution_convert_fusion
  177.1 1.0 copy.67
  178.0 3.5 all-to-all-start.1
  181.5 10.1 %all-to-all-done.1 = bf16[8,64,512]{2,1,0:T(8,128)(2,1)S(1)} async-done(((bf16[8,64,512]{2,1,0:T(8,128)(2,1)}), bf16[8,64,512]{2,1,0:T(8,128)(2,1)S(1)}, u32[]{:S(2)}, u32[]{:S(2)}) %all-to-all-start.1) | async-done | bytes 524320 | tf_op jit(solution)/shard_map/while/body/eval_jaxpr/all_to_all | solution.py:44
  191.7 1.3 collective-permute-start
  193.0 0.9 select_dynamic-update-slice_fusion.5
  194.0 0.8 broadcast_in_dim.44
  194.9 3.5 all-to-all-start
  198.4 12.2 %all-to-all-done = bf16[8,64,512]{2,1,0:T(8,128)(2,1)S(1)} async-done(((bf16[8,64,512]{2,1,0:T(8,128)(2,1)}), bf16[8,64,512]{2,1,0:T(8,128)(2,1)S(1)}, u32[]{:S(2)}, u32[]{:S(2)}) %all-to-all-start) | async-done | bytes 524320 | tf_op jit(solution)/shard_map/while/body/eval_jaxpr/all_to_all | solution.py:28
  211.2 2.1 copy-done
  213.3 4.5 %conditional.2 = (bf16[64,640]{1,0:T(8,128)(2,1)}, bf16[64,4096]{1,0:T(8,128)(2,1)S(1)}) conditional(s32[]{:T(128)} %convert_element_type.313, () %tuple.49, (bf16[64,4096]{1,0:T(8,128)(2,1)S(1)}, bf16[4096,640]{1,0:T(8,128)(2,1)S(1)}, bf16[640,4096]{1,0:T(8,128)(2,1)}) %tuple.63), branch_computations={%region_2.2_spmd, %region_3.3_spmd} | conditional | flops 671719424 | bytes 32669740 | solution.py:94
  213.3 1.7 fusion.7
  215.0 0.9 copy-done.1
  215.8 1.9 convolution_convert_fusion
  218.0 1.0 copy.67
  218.9 3.5 all-to-all-start.1
  222.4 11.1 %all-to-all-done.1 = bf16[8,64,512]{2,1,0:T(8,128)(2,1)S(1)} async-done(((bf16[8,64,512]{2,1,0:T(8,128)(2,1)}), bf16[8,64,512]{2,1,0:T(8,128)(2,1)S(1)}, u32[]{:S(2)}, u32[]{:S(2)}) %all-to-all-start.1) | async-done | bytes 524320 | tf_op jit(solution)/shard_map/while/body/eval_jaxpr/all_to_all | solution.py:44
  233.7 1.3 collective-permute-start
  235.0 0.9 select_dynamic-update-slice_fusion.5
  236.0 0.8 broadcast_in_dim.44
  236.8 3.5 all-to-all-start
  240.3 12.2 %all-to-all-done = bf16[8,64,512]{2,1,0:T(8,128)(2,1)S(1)} async-done(((bf16[8,64,512]{2,1,0:T(8,128)(2,1)}), bf16[8,64,512]{2,1,0:T(8,128)(2,1)S(1)}, u32[]{:S(2)}, u32[]{:S(2)}) %all-to-all-start) | async-done | bytes 524320 | tf_op jit(solution)/shard_map/while/body/eval_jaxpr/all_to_all | solution.py:28
  253.2 2.1 copy-done
  255.2 0.7 conditional.2
  255.2 0.6 broadcast.38
  256.1 1.0 copy.67
  257.1 3.5 all-to-all-start.1
  260.6 11.1 %all-to-all-done.1 = bf16[8,64,512]{2,1,0:T(8,128)(2,1)S(1)} async-done(((bf16[8,64,512]{2,1,0:T(8,128)(2,1)}), bf16[8,64,512]{2,1,0:T(8,128)(2,1)S(1)}, u32[]{:S(2)}, u32[]{:S(2)}) %all-to-all-start.1) | async-done | bytes 524320 | tf_op jit(solution)/shard_map/while/body/eval_jaxpr/all_to_all | solution.py:44
  271.7 3.6 collective-permute-start
  275.5 0.8 collective-permute-done
  276.3 0.7 copy-done.2
  277.0 0.7 copy.43
  277.7 38.9 %all_to_all.38 = bf16[128,16,256]{0,2,1:T(8,128)(2,1)S(1)} all-to-all(bf16[128,16,256]{0,2,1:T(8,128)(2,1)S(1)} %bitcast.112), channel_id=1, replica_groups=mesh['section'=2,'dp_0'=8,'dp_1'=2,'tensor'=8] {'dp_0','dp_1'}, dimensions={1} | all-to-all | bytes 2097152 | tf_op jit(solution)/shard_map/all_to_all | solution.py:119
  316.5 43.1 %all-gather.9.cloned.1.call-done = bf16[2048,640]{1,0:T(8,128)(2,1)} async-done(((bf16[128,640]{1,0:T(8,128)(2,1)}), bf16[2048,640]{1,0:T(8,128)(2,1)}) %all-gather.9.cloned.1.call-update) | async-done | bytes 2621456 | tf_op jit(solution)/shard_map/all_gather | solution.py:118
  359.7 1.3 convolution_convert_fusion.1
  361.0 1.2 convolution_convert_fusion.2
  362.2 1.2 convolution_convert_fusion.3
  363.4 1.2 convolution_convert_fusion.4
  364.6 1.2 convolution_convert_fusion.5
  365.9 0.3 convolution_convert_fusion.6
  366.1 0.3 convolution_convert_fusion.7
  366.4 0.3 convolution_convert_fusion.8
  366.7 0.3 convolution_convert_fusion.9
  367.0 0.3 convolution_convert_fusion.10
  367.3 0.3 convolution_convert_fusion.11
  367.6 0.3 convolution_convert_fusion.12
  367.9 0.3 convolution_convert_fusion.13
  368.1 0.3 convolution_convert_fusion.14
  368.4 0.3 convolution_convert_fusion.16
  368.7 0.3 convolution_convert_fusion.15
  369.0 1.5 fusion.9
  (60 shorter events, 3.1 us)
Async XLA Ops:
  7.2 21.8 %copy-start.7 = (bf16[1,512]{1,0:T(2,128)(2,1)S(1)}, bf16[1,512]{1,0:T(2,128)(2,1)}, u32[]{:S(2)}) copy-start(bf16[1,512]{1,0:T(2,128)(2,1)} %param.10) | copy-start | bytes 3076
  7.2 144.4 %copy-start.6 = (bf16[128,512]{1,0:T(8,128)(2,1)S(1)}, bf16[128,512]{1,0:T(8,128)(2,1)}, u32[]{:S(2)}) copy-start(bf16[128,512]{1,0:T(8,128)(2,1)} %param.9) | copy-start | bytes 393220
  7.2 79.3 %all-gather.11.cloned.1.call-start = ((), (), s32[]{:S(2)}) async-start(), calls=%async_computation.4 | async-start | bytes 5898240 | tf_op jit(solution)/shard_map/all_gather | solution.py:16
  17.7 133.8 %all-gather.13.cloned.1.call-start = ((), (), s32[]{:S(2)}) async-start(), calls=%async_computation.5 | async-start | bytes 5898240 | tf_op jit(solution)/shard_map/all_gather | solution.py:16
  28.9 330.8 %all-gather.9.cloned.1.call-start = ((), (), s32[]{:S(2)}) async-start(), calls=%async_computation.3 | async-start | bytes 2785280 | tf_op jit(solution)/shard_map/all_gather | solution.py:118
  151.5 125.4 %copy-start.5 = (bf16[1,128,4096]{2,1,0:T(8,128)(2,1)S(1)}, bf16[1,128,4096]{2,1,0:T(8,128)(2,1)}, u32[]{:S(2)}) copy-start(bf16[1,128,4096]{2,1,0:T(8,128)(2,1)} %param.13) | copy-start | bytes 3145732
  152.5 17.2 %all-to-all-start = ((bf16[8,64,512]{2,1,0:T(8,128)(2,1)}), bf16[8,64,512]{2,1,0:T(8,128)(2,1)S(1)}, u32[]{:S(2)}, u32[]{:S(2)}) async-start(bf16[8,64,512]{2,1,0:T(8,128)(2,1)} %broadcast_in_dim.44), calls=%async_computation | async-start | bytes 1048576 | tf_op jit(solution)/shard_map/while/body/eval_jaxpr/all_to_all | solution.py:28
  169.9 2.5 copy-start
  172.4 2.5 copy-start.1
  178.0 13.6 %all-to-all-start.1 = ((bf16[8,64,512]{2,1,0:T(8,128)(2,1)}), bf16[8,64,512]{2,1,0:T(8,128)(2,1)S(1)}, u32[]{:S(2)}, u32[]{:S(2)}) async-start(bf16[8,64,512]{2,1,0:T(8,128)(2,1)} %copy.67), calls=%async_computation.1 | async-start | bytes 1048576 | tf_op jit(solution)/shard_map/while/body/eval_jaxpr/all_to_all | solution.py:44
  191.7 2.2 collective-permute-start
  194.9 15.7 %all-to-all-start = ((bf16[8,64,512]{2,1,0:T(8,128)(2,1)}), bf16[8,64,512]{2,1,0:T(8,128)(2,1)S(1)}, u32[]{:S(2)}, u32[]{:S(2)}) async-start(bf16[8,64,512]{2,1,0:T(8,128)(2,1)} %broadcast_in_dim.44), calls=%async_computation | async-start | bytes 1048576 | tf_op jit(solution)/shard_map/while/body/eval_jaxpr/all_to_all | solution.py:28
  210.8 2.5 copy-start
  213.3 2.5 copy-start.1
  218.9 14.6 %all-to-all-start.1 = ((bf16[8,64,512]{2,1,0:T(8,128)(2,1)}), bf16[8,64,512]{2,1,0:T(8,128)(2,1)S(1)}, u32[]{:S(2)}, u32[]{:S(2)}) async-start(bf16[8,64,512]{2,1,0:T(8,128)(2,1)} %copy.67), calls=%async_computation.1 | async-start | bytes 1048576 | tf_op jit(solution)/shard_map/while/body/eval_jaxpr/all_to_all | solution.py:44
  233.7 2.2 collective-permute-start
  236.8 15.7 %all-to-all-start = ((bf16[8,64,512]{2,1,0:T(8,128)(2,1)}), bf16[8,64,512]{2,1,0:T(8,128)(2,1)S(1)}, u32[]{:S(2)}, u32[]{:S(2)}) async-start(bf16[8,64,512]{2,1,0:T(8,128)(2,1)} %broadcast_in_dim.44), calls=%async_computation | async-start | bytes 1048576 | tf_op jit(solution)/shard_map/while/body/eval_jaxpr/all_to_all | solution.py:28
  252.8 2.5 copy-start
  257.1 14.6 %all-to-all-start.1 = ((bf16[8,64,512]{2,1,0:T(8,128)(2,1)}), bf16[8,64,512]{2,1,0:T(8,128)(2,1)S(1)}, u32[]{:S(2)}, u32[]{:S(2)}) async-start(bf16[8,64,512]{2,1,0:T(8,128)(2,1)} %copy.67), calls=%async_computation.1 | async-start | bytes 1048576 | tf_op jit(solution)/shard_map/while/body/eval_jaxpr/all_to_all | solution.py:44
  271.7 4.5 %collective-permute-start = (bf16[64,512]{1,0:T(8,128)(2,1)S(1)}, bf16[64,512]{1,0:T(8,128)(2,1)S(1)}, u32[]{:S(2)}, u32[]{:S(2)}) collective-permute-start(bf16[64,512]{1,0:T(8,128)(2,1)S(1)} %get-tuple-element.299), channel_id=1, source_target_pairs={{0,128},{1,129},{2,130},{3,131},{4,132},{5,133},{6,134},{7,135},{8... | collective-permute-start | bytes 196616 | tf_op jit(solution)/shard_map/while/body/eval_jaxpr/ppermute | solution.py:51
  276.3 0.7 copy-start.2
  276.3 86.0 %copy-start.4 = (bf16[128,512]{1,0:T(8,128)(2,1)}, bf16[128,512]{1,0:T(8,128)(2,1)S(1)}, u32[]{:S(2)}) copy-start(bf16[128,512]{1,0:T(8,128)(2,1)S(1)} %get-tuple-element.209) | copy-start | bytes 393220
  359.7 6.2 %copy-start.3 = (bf16[2048,640]{1,0:T(8,128)(2,1)S(1)}, bf16[2048,640]{1,0:T(8,128)(2,1)}, u32[]{:S(2)}) copy-start(bf16[2048,640]{1,0:T(8,128)(2,1)} %all-gather.9.cloned.1.call-done) | copy-start | bytes 7864324
Sparse Core Ops, SparseCore 0:
  17.8 68.6 all-gather.10
  88.3 63.1 all-gather.12
  277.1 82.5 all-gather.8
where the time goes:
time: 378 us; the launch traced here: 377 us
  waiting for transfers between devices  203 us (54%)
  blocking collectives  92.1 us (24%)
  starting transfers between devices  29.6 us (8%)
  matrix products  16.4 us (4%)
  local copies, waits for them, and re-layouts  16.2 us (4%)
  between operations  14 us (4%)
  other arithmetic  5.33 us (1%)
    all_gather x2, waiting for transfers between devices, gathered_by_axis(): filled = lax.all_gather(filled, axes[number], axis=dim, tiled=True)  90.9 us
    all_gather x1, waiting for transfers between devices, body(): hidden_all = lax.all_gather(hiddens, DP, axis=0, tiled=True)  43.1 us
    all_to_all x1, blocking collectives, body(): lax.all_to_all(cot_own, DP, split_axis=1, concat_axis=0, tiled=True)  38.9 us
    all_to_all x3, waiting for transfers between devices, copy_for_each(): lax.all_to_all(jnp.broadcast_to(array[None], (peers, *array.shape)), axis...  35.8 us
    all_to_all x3, waiting for transfers between devices, summed_on_arrival(): lax.all_to_all(pieces, axis, split_axis=0, concat_axis=0, tiled=True)  32.3 us
    all_gather x1, blocking collectives, body(): gain_whole = lax.all_gather(gain_own, 'tensor', axis=0, tiled=True)  31.6 us
    all_gather x2, blocking collectives, gathered_by_axis(): filled = lax.all_gather(filled, axes[number], axis=dim, tiled=True)  21.6 us
    all_to_all x3, starting transfers between devices, copy_for_each(): lax.all_to_all(jnp.broadcast_to(array[None], (peers, *array.shape)), axis...  12.8 us
  transfers between devices with their start and end apart: 12, of which 10 were waited for; matrix products, arithmetic and copies ran while one was open for 1% of the time, Pallas kernels for 0%

commit v1 on v0

--- a/solution.py
+++ b/solution.py
@@ -115,7 +115,10 @@
     hiddens = final_state[2]
     cot_own = cotangent[0]
     dp_count = lax.axis_size(DP)
-    hidden_all = lax.all_gather(hiddens, DP, axis=0, tiled=True)
+    front = lax.axis_size(DP)
+    v_next = jnp.stack([hiddens] * front, axis=0)
+    b_now = lax.all_to_all(v_next, DP, 0, 0)
+    hidden_all = jnp.concatenate(b_now, axis=0)
     cot_mine = lax.all_to_all(cot_own, DP, split_axis=1, concat_axis=0, tiled=True)
     grad_own = jnp.zeros((hidden_width, width // dp_count), jnp.float32)
     for peer_id in range(dp_count):

time: 378 us -> 381 us (level)
  waiting for transfers between devices: 203 us -> 171 us
  blocking collectives: 92.1 us -> 120 us
  starting transfers between devices: 29.6 us -> 40.1 us
  matrix products: 16.4 us -> 11.7 us
    all_gather x1 -> x0, waiting for transfers between devices: 43.1 us -> none  [body(): hidden_all = lax.all_gather(hiddens, DP, axis=0, tiled=True)]
    all_to_all x1, blocking collectives: 38.9 us -> 67.5 us  [body(): b_now = lax.all_to_all(v_next, DP, 0, 0)]
    all_to_all x0 -> x1, starting transfers between devices: none -> 10.5 us  [body(): lax.all_to_all(cot_own, DP, split_axis=1, concat_axis=0, tiled=True)]
    all_to_all x0 -> x1, waiting for transfers between devices: none -> 6.2 us  [body(): lax.all_to_all(cot_own, DP, split_axis=1, concat_axis=0, tiled=True)]
    all_gather x2, waiting for transfers between devices: 90.9 us -> 95.8 us  [gathered_by_axis(): filled = lax.all_gather(filled, axes[number], axis=dim, tiled=True)]
    dot_general x16, matrix products: 9.16 us -> 4.46 us  [body(): lax.dot_general(hidden_all[lower:lower + tok_rows], cot_mine[lower:lower...]
where the time goes in v1:
time: 381 us; the launch traced here: 379 us
  waiting for transfers between devices  171 us (45%)
  blocking collectives  120 us (31%)
  starting transfers between devices  40.1 us (11%)
  local copies, waits for them, and re-layouts  16.5 us (4%)
  between operations  14.2 us (4%)
  matrix products  11.7 us (3%)
  other arithmetic  5.25 us (1%)
    all_gather x2, waiting for transfers between devices, gathered_by_axis(): filled = lax.all_gather(filled, axes[number], axis=dim, tiled=True)  95.8 us
    all_to_all x1, blocking collectives, body(): b_now = lax.all_to_all(v_next, DP, 0, 0)  67.5 us
    all_to_all x3, waiting for transfers between devices, copy_for_each(): lax.all_to_all(jnp.broadcast_to(array[None], (peers, *array.shape)), axis...  35.8 us
    all_to_all x3, waiting for transfers between devices, summed_on_arrival(): lax.all_to_all(pieces, axis, split_axis=0, concat_axis=0, tiled=True)  32.3 us
    all_gather x1, blocking collectives, body(): gain_whole = lax.all_gather(gain_own, 'tensor', axis=0, tiled=True)  31.1 us
    all_gather x2, blocking collectives, gathered_by_axis(): filled = lax.all_gather(filled, axes[number], axis=dim, tiled=True)  21.7 us
    all_to_all x3, starting transfers between devices, copy_for_each(): lax.all_to_all(jnp.broadcast_to(array[None], (peers, *array.shape)), axis...  12.8 us
    all_to_all x1, starting transfers between devices, body(): lax.all_to_all(cot_own, DP, split_axis=1, concat_axis=0, tiled=True)  10.5 us
  transfers between devices with their start and end apart: 12, of which 10 were waited for; matrix products, arithmetic and copies ran while one was open for 1% of the time, Pallas kernels for 0%

profile of v1, /device:TPU:2, one launch (start us, length us, event | category | flops | bytes accessed | tf_op | source)
XLA Modules:
  0.0 379.5 jit_solution(14249435148735154991)
XLA Ops:
  7.2 10.6 %all-gather.1 = bf16[1,512,640]{2,1,0:T(8,128)(2,1)} all-gather(bf16[1,256,640]{2,1,0:T(8,128)(2,1)} %param.11), channel_id=3, replica_groups=mesh['section'=2,'dp_0'=8,'dp_1'=2,'tensor'=8] {'dp_1'}, dimensions={1}, use_global_device_ids=true | all-gather | bytes 983040 | tf_op jit(solution)/shard_map/all_gather | solution.py:16
  17.9 11.1 %all-gather.3 = bf16[1,640,512]{2,1,0:T(8,128)(2,1)} all-gather(bf16[1,640,256]{2,1,0:T(8,128)(2,1)} %param.12), channel_id=5, replica_groups=mesh['section'=2,'dp_0'=8,'dp_1'=2,'tensor'=8] {'dp_1'}, dimensions={2}, use_global_device_ids=true | all-gather | bytes 983040 | tf_op jit(solution)/shard_map/all_gather | solution.py:16
  29.0 1.3 copy.43
  30.3 10.5 %all-to-all-start.3 = ((bf16[128,16,256]{0,2,1:T(8,128)(2,1)}), bf16[128,16,256]{0,2,1:T(8,128)(2,1)S(1)}, u32[]{:S(2)}, u32[]{:S(2)}) async-start(bf16[128,16,256]{0,2,1:T(8,128)(2,1)} %bitcast.6), calls=%async_computation.3 | async-start | bytes 2097152 | tf_op jit(solution)/shard_map/all_to_all | solution.py:122
  40.9 31.1 %all-gather = bf16[1,4096]{1,0:T(2,128)(2,1)S(1)} all-gather(bf16[1,512]{1,0:T(2,128)(2,1)S(1)} %copy-done.5), channel_id=2, replica_groups=mesh['section'=2,'dp_0'=8,'dp_1'=2,'tensor'=8] {'tensor'}, dimensions={1}, use_global_device_ids=true | all-gather | bytes 9216 | tf_op jit(solution)/shard_map/all_gather | solution.py:62
  72.1 6.2 %all-to-all-done.3 = bf16[128,16,256]{0,2,1:T(8,128)(2,1)S(1)} async-done(((bf16[128,16,256]{0,2,1:T(8,128)(2,1)}), bf16[128,16,256]{0,2,1:T(8,128)(2,1)S(1)}, u32[]{:S(2)}, u32[]{:S(2)}) %all-to-all-start.3) | async-done | bytes 1048608 | tf_op jit(solution)/shard_map/all_to_all | solution.py:122
  78.3 30.8 %all-gather.8.cloned.1.call-done = bf16[1,4096,640]{2,1,0:T(8,128)(2,1)} async-done(((bf16[1,512,640]{2,1,0:T(8,128)(2,1)}), bf16[1,4096,640]{2,1,0:T(8,128)(2,1)}) %all-gather.8.cloned.1.call-update) | async-done | bytes 5242896 | tf_op jit(solution)/shard_map/all_gather | solution.py:16
  109.1 65.0 %all-gather.10.cloned.1.call-done = bf16[1,640,4096]{2,1,0:T(8,128)(2,1)} async-done(((bf16[1,640,512]{2,1,0:T(8,128)(2,1)}), bf16[1,640,4096]{2,1,0:T(8,128)(2,1)}) %all-gather.10.cloned.1.call-update) | async-done | bytes 5242896 | tf_op jit(solution)/shard_map/all_gather | solution.py:16
  174.1 124.7 %while.18 = (s32[]{:T(128)}, bf16[64,512]{1,0:T(8,128)(2,1)S(1)}, bf16[128,512]{1,0:T(8,128)(2,1)S(1)}, bf16[128,640]{1,0:T(8,128)(2,1)S(1)}, pred[]{:T(512)}, /...) while((s32[]{:T(128)}, bf16[64,512]{1,0:T(8,128)(2,1)S(1)}, ...), condition=%wide.region_5.6_spmd, body=%wide.region_0.5_spmd.sunk | while | flops 674254912 | bytes 67036620 | solution.py:113
  174.2 0.8 broadcast_in_dim.44
  175.0 5.8 %all-to-all-start = ((bf16[8,64,512]{2,1,0:T(8,128)(2,1)}), bf16[8,64,512]{2,1,0:T(8,128)(2,1)S(1)}, u32[]{:S(2)}, u32[]{:S(2)}) async-start(bf16[8,64,512]{2,1,0:T(8,128)(2,1)} %broadcast_in_dim.44), calls=%async_computation | async-start | bytes 1048576 | tf_op jit(solution)/shard_map/while/body/eval_jaxpr/all_to_all | solution.py:28
  180.9 11.4 %all-to-all-done = bf16[8,64,512]{2,1,0:T(8,128)(2,1)S(1)} async-done(((bf16[8,64,512]{2,1,0:T(8,128)(2,1)}), bf16[8,64,512]{2,1,0:T(8,128)(2,1)S(1)}, u32[]{:S(2)}, u32[]{:S(2)}) %all-to-all-start) | async-done | bytes 524320 | tf_op jit(solution)/shard_map/while/body/eval_jaxpr/all_to_all | solution.py:28
  192.9 2.1 copy-done
  195.0 4.5 %conditional.2 = (bf16[64,640]{1,0:T(8,128)(2,1)}, bf16[64,4096]{1,0:T(8,128)(2,1)S(1)}) conditional(s32[]{:T(128)} %convert_element_type.313, () %tuple.49, (bf16[64,4096]{1,0:T(8,128)(2,1)S(1)}, bf16[4096,640]{1,0:T(8,128)(2,1)S(1)}, bf16[640,4096]{1,0:T(8,128)(2,1)}) %tuple.61), branch_computations={%region_2.2_spmd, %region_3.3_spmd} | conditional | flops 671719424 | bytes 32669740 | solution.py:94
  195.0 1.7 fusion.7
  196.6 0.8 copy-done.1
  197.5 1.9 convolution_convert_fusion
  199.6 1.0 copy.67
  200.6 3.5 all-to-all-start.1
  204.1 10.1 %all-to-all-done.1 = bf16[8,64,512]{2,1,0:T(8,128)(2,1)S(1)} async-done(((bf16[8,64,512]{2,1,0:T(8,128)(2,1)}), bf16[8,64,512]{2,1,0:T(8,128)(2,1)S(1)}, u32[]{:S(2)}, u32[]{:S(2)}) %all-to-all-start.1) | async-done | bytes 524320 | tf_op jit(solution)/shard_map/while/body/eval_jaxpr/all_to_all | solution.py:44
  214.3 1.3 collective-permute-start
  215.6 0.9 select_dynamic-update-slice_fusion.5
  216.6 0.8 broadcast_in_dim.44
  217.5 3.5 all-to-all-start
  221.0 12.2 %all-to-all-done = bf16[8,64,512]{2,1,0:T(8,128)(2,1)S(1)} async-done(((bf16[8,64,512]{2,1,0:T(8,128)(2,1)}), bf16[8,64,512]{2,1,0:T(8,128)(2,1)S(1)}, u32[]{:S(2)}, u32[]{:S(2)}) %all-to-all-start) | async-done | bytes 524320 | tf_op jit(solution)/shard_map/while/body/eval_jaxpr/all_to_all | solution.py:28
  233.8 2.1 copy-done
  235.9 4.5 %conditional.2 = (bf16[64,640]{1,0:T(8,128)(2,1)}, bf16[64,4096]{1,0:T(8,128)(2,1)S(1)}) conditional(s32[]{:T(128)} %convert_element_type.313, () %tuple.49, (bf16[64,4096]{1,0:T(8,128)(2,1)S(1)}, bf16[4096,640]{1,0:T(8,128)(2,1)S(1)}, bf16[640,4096]{1,0:T(8,128)(2,1)}) %tuple.61), branch_computations={%region_2.2_spmd, %region_3.3_spmd} | conditional | flops 671719424 | bytes 32669740 | solution.py:94
  235.9 1.7 fusion.7
  237.6 0.9 copy-done.1
  238.4 1.9 convolution_convert_fusion
  240.6 1.0 copy.67
  241.5 3.5 all-to-all-start.1
  245.0 11.1 %all-to-all-done.1 = bf16[8,64,512]{2,1,0:T(8,128)(2,1)S(1)} async-done(((bf16[8,64,512]{2,1,0:T(8,128)(2,1)}), bf16[8,64,512]{2,1,0:T(8,128)(2,1)S(1)}, u32[]{:S(2)}, u32[]{:S(2)}) %all-to-all-start.1) | async-done | bytes 524320 | tf_op jit(solution)/shard_map/while/body/eval_jaxpr/all_to_all | solution.py:44
  256.2 1.3 collective-permute-start
  257.5 0.9 select_dynamic-update-slice_fusion.5
  258.5 0.8 broadcast_in_dim.44
  259.4 3.5 all-to-all-start
  262.9 12.2 %all-to-all-done = bf16[8,64,512]{2,1,0:T(8,128)(2,1)S(1)} async-done(((bf16[8,64,512]{2,1,0:T(8,128)(2,1)}), bf16[8,64,512]{2,1,0:T(8,128)(2,1)S(1)}, u32[]{:S(2)}, u32[]{:S(2)}) %all-to-all-start) | async-done | bytes 524320 | tf_op jit(solution)/shard_map/while/body/eval_jaxpr/all_to_all | solution.py:28
  275.7 2.1 copy-done
  277.8 0.7 conditional.2
  277.8 0.6 broadcast.40
  278.7 1.0 copy.67
  279.6 3.5 all-to-all-start.1
  283.1 11.1 %all-to-all-done.1 = bf16[8,64,512]{2,1,0:T(8,128)(2,1)S(1)} async-done(((bf16[8,64,512]{2,1,0:T(8,128)(2,1)}), bf16[8,64,512]{2,1,0:T(8,128)(2,1)S(1)}, u32[]{:S(2)}, u32[]{:S(2)}) %all-to-all-start.1) | async-done | bytes 524320 | tf_op jit(solution)/shard_map/while/body/eval_jaxpr/all_to_all | solution.py:44
  294.3 3.6 collective-permute-start
  298.0 0.8 collective-permute-done
  298.9 0.3 stack.2
  299.2 67.5 %all_to_all.43 = bf16[16,128,640]{2,1,0:T(8,128)(2,1)S(1)} all-to-all(bf16[16,128,640]{2,1,0:T(8,128)(2,1)S(1)} %stack.2), channel_id=1, replica_groups=mesh['section'=2,'dp_0'=8,'dp_1'=2,'tensor'=8] {'dp_0','dp_1'}, dimensions={0} | all-to-all | bytes 5242880 | tf_op jit(solution)/shard_map/all_to_all | solution.py:120
  366.7 0.3 convolution_convert_fusion.1
  366.9 0.3 convolution_convert_fusion.2
  367.2 0.3 convolution_convert_fusion.3
  367.5 0.3 convolution_convert_fusion.4
  367.8 0.3 convolution_convert_fusion.5
  368.1 0.3 convolution_convert_fusion.6
  368.4 0.3 convolution_convert_fusion.7
  368.7 0.3 convolution_convert_fusion.8
  368.9 0.3 convolution_convert_fusion.9
  369.2 0.3 convolution_convert_fusion.10
  369.5 0.3 convolution_convert_fusion.11
  369.8 0.3 convolution_convert_fusion.12
  370.1 0.3 convolution_convert_fusion.13
  370.4 0.3 convolution_convert_fusion.14
  370.7 0.3 convolution_convert_fusion.16
  371.2 1.4 fusion.9
  (56 shorter events, 3.3 us)
Async XLA Ops:
  7.2 21.9 %copy-start.3 = (bf16[1,128,4096]{2,1,0:T(8,128)(2,1)S(1)}, bf16[1,128,4096]{2,1,0:T(8,128)(2,1)}, u32[]{:S(2)}) copy-start(bf16[1,128,4096]{2,1,0:T(8,128)(2,1)} %param.13) | copy-start | bytes 3145732
  7.2 101.9 %all-gather.8.cloned.1.call-start = ((), (), s32[]{:S(2)}) async-start(), calls=%async_computation.4 | async-start | bytes 5898240 | tf_op jit(solution)/shard_map/all_gather | solution.py:16
  17.8 156.3 %all-gather.10.cloned.1.call-start = ((), (), s32[]{:S(2)}) async-start(), calls=%async_computation.5 | async-start | bytes 5898240 | tf_op jit(solution)/shard_map/all_gather | solution.py:16
  29.0 11.9 %copy-start.5 = (bf16[1,512]{1,0:T(2,128)(2,1)S(1)}, bf16[1,512]{1,0:T(2,128)(2,1)}, u32[]{:S(2)}) copy-start(bf16[1,512]{1,0:T(2,128)(2,1)} %param.10) | copy-start | bytes 3076
  29.0 145.1 %copy-start.4 = (bf16[128,512]{1,0:T(8,128)(2,1)S(1)}, bf16[128,512]{1,0:T(8,128)(2,1)}, u32[]{:S(2)}) copy-start(bf16[128,512]{1,0:T(8,128)(2,1)} %param.9) | copy-start | bytes 393220
  30.3 47.9 %all-to-all-start.3 = ((bf16[128,16,256]{0,2,1:T(8,128)(2,1)}), bf16[128,16,256]{0,2,1:T(8,128)(2,1)S(1)}, u32[]{:S(2)}, u32[]{:S(2)}) async-start(bf16[128,16,256]{0,2,1:T(8,128)(2,1)} %bitcast.6), calls=%async_computation.3 | async-start | bytes 2097152 | tf_op jit(solution)/shard_map/all_to_all | solution.py:122
  175.0 17.2 %all-to-all-start = ((bf16[8,64,512]{2,1,0:T(8,128)(2,1)}), bf16[8,64,512]{2,1,0:T(8,128)(2,1)S(1)}, u32[]{:S(2)}, u32[]{:S(2)}) async-start(bf16[8,64,512]{2,1,0:T(8,128)(2,1)} %broadcast_in_dim.44), calls=%async_computation | async-start | bytes 1048576 | tf_op jit(solution)/shard_map/while/body/eval_jaxpr/all_to_all | solution.py:28
  192.5 2.5 copy-start
  195.0 2.5 copy-start.1
  200.6 13.6 %all-to-all-start.1 = ((bf16[8,64,512]{2,1,0:T(8,128)(2,1)}), bf16[8,64,512]{2,1,0:T(8,128)(2,1)S(1)}, u32[]{:S(2)}, u32[]{:S(2)}) async-start(bf16[8,64,512]{2,1,0:T(8,128)(2,1)} %copy.67), calls=%async_computation.1 | async-start | bytes 1048576 | tf_op jit(solution)/shard_map/while/body/eval_jaxpr/all_to_all | solution.py:44
  214.3 2.2 collective-permute-start
  217.5 15.7 %all-to-all-start = ((bf16[8,64,512]{2,1,0:T(8,128)(2,1)}), bf16[8,64,512]{2,1,0:T(8,128)(2,1)S(1)}, u32[]{:S(2)}, u32[]{:S(2)}) async-start(bf16[8,64,512]{2,1,0:T(8,128)(2,1)} %broadcast_in_dim.44), calls=%async_computation | async-start | bytes 1048576 | tf_op jit(solution)/shard_map/while/body/eval_jaxpr/all_to_all | solution.py:28
  233.4 2.5 copy-start
  235.9 2.5 copy-start.1
  241.5 14.6 %all-to-all-start.1 = ((bf16[8,64,512]{2,1,0:T(8,128)(2,1)}), bf16[8,64,512]{2,1,0:T(8,128)(2,1)S(1)}, u32[]{:S(2)}, u32[]{:S(2)}) async-start(bf16[8,64,512]{2,1,0:T(8,128)(2,1)} %copy.67), calls=%async_computation.1 | async-start | bytes 1048576 | tf_op jit(solution)/shard_map/while/body/eval_jaxpr/all_to_all | solution.py:44
  256.2 2.2 collective-permute-start
  259.4 15.7 %all-to-all-start = ((bf16[8,64,512]{2,1,0:T(8,128)(2,1)}), bf16[8,64,512]{2,1,0:T(8,128)(2,1)S(1)}, u32[]{:S(2)}, u32[]{:S(2)}) async-start(bf16[8,64,512]{2,1,0:T(8,128)(2,1)} %broadcast_in_dim.44), calls=%async_computation | async-start | bytes 1048576 | tf_op jit(solution)/shard_map/while/body/eval_jaxpr/all_to_all | solution.py:28
  275.3 2.5 copy-start
  279.6 14.6 %all-to-all-start.1 = ((bf16[8,64,512]{2,1,0:T(8,128)(2,1)}), bf16[8,64,512]{2,1,0:T(8,128)(2,1)S(1)}, u32[]{:S(2)}, u32[]{:S(2)}) async-start(bf16[8,64,512]{2,1,0:T(8,128)(2,1)} %copy.67), calls=%async_computation.1 | async-start | bytes 1048576 | tf_op jit(solution)/shard_map/while/body/eval_jaxpr/all_to_all | solution.py:44
  294.3 4.5 %collective-permute-start = (bf16[64,512]{1,0:T(8,128)(2,1)S(1)}, bf16[64,512]{1,0:T(8,128)(2,1)S(1)}, u32[]{:S(2)}, u32[]{:S(2)}) collective-permute-start(bf16[64,512]{1,0:T(8,128)(2,1)S(1)} %get-tuple-element.299), channel_id=1, source_target_pairs={{0,128},{1,129},{2,130},{3,131},{4,132},{5,133},{6,134},{7,135},{8... | collective-permute-start | bytes 196616 | tf_op jit(solution)/shard_map/while/body/eval_jaxpr/ppermute | solution.py:51
  298.9 67.8 %copy-start.2 = (bf16[128,512]{1,0:T(8,128)(2,1)}, bf16[128,512]{1,0:T(8,128)(2,1)S(1)}, u32[]{:S(2)}) copy-start(bf16[128,512]{1,0:T(8,128)(2,1)S(1)} %get-tuple-element.209) | copy-start | bytes 393220
Sparse Core Ops, SparseCore 0:
  17.9 91.0 all-gather.7
  110.9 63.1 all-gather.9
